TPU v7x, 32 devices: a whole 2x2x4 slice. The times are simulated.
32 devices in a mesh: job: 2 (over y), row: 4 (over z), col: 2 (over x), samp: 2 (over core).
Axes of the slice: x: 2, y: 2, z: 4, core: 2. Of those that a mesh axis runs over, the one named last changes fastest.
Arguments:
- pair_repr: bfloat16 [256, 128, 128], P(('job', 'row'), ('col', 'samp')), parts along dimension 0, may hold values from -100 to 100
- asym_id: int32 [256], P('job'), parts along dimension 0, may hold values from 0 to 7, never falling along the last dimension, each value on 1 to 32 neighbouring positions
- valid_len: int32 [2], P('job'), parts along dimension 0, may hold values from 64 to 128
- rel_embed: bfloat16 [128, 128], replicated, may hold values from -12 to 12
- pair_gain: float32 [128], replicated, may hold values from 0.25 to 1.75
- bias_weight: bfloat16 [128, 16], replicated, may hold values from -64 to 64
- tokens: bfloat16 [32, 128, 768], P(('job', 'col', 'samp'), 'row'), parts along dimension 0, may hold values from -6 to 6
- token_gain: float32 [1, 768], replicated, may hold values from 0.25 to 1.75
- qkv_weight: bfloat16 [1, 3, 768, 768], P(None, None, None, 'row'), may hold values from -0.21875 to 0.21875
- out_weight: bfloat16 [1, 768, 768], P(None, 'row'), may hold values from -0.21875 to 0.21875
Outputs:
- refined: bfloat16 [32, 128, 768], P(('job', 'col', 'samp'), 'row'), parts along dimension 0
There are 2 independent parts, one for each index of `job`. A program takes and returns all parts, laid end to end along the dimension named above; an argument that names none is the same for every part. Nothing has to cross between parts.
Inputs may be any that keep to these rules, and one draw needn't show every extreme that they name: `asym_id`: chain indices never fall along the tokens.
All inputs are finite; a program needn't handle non-finite values.
Results may differ from a plain program's by a relative error of at most 0.002.
The roundings to bfloat16 on the way count: a program that leaves them out, or rounds other values in their place, can miss the bound.
Values may be sent and summed in bfloat16 or wider, within the bound.
A program may use at most 64 MiB of HBM per device.

v0:
```python
import math
import jax
import jax.numpy as jnp
from jax import lax
from jax.sharding import PartitionSpec as P

HEAD_DIM = 48
epsilon = 1e-05


def normalize(values, gain_vector):
    average = jnp.mean(values, axis=-1, keepdims=True)
    centered = values - average
    variance = jnp.mean(centered * centered, axis=-1, keepdims=True)
    return centered * lax.rsqrt(variance + epsilon) * gain_vector


def bias_tile_of(pair_repr, asym_id, rel_embed, pair_gain, bias_weight):
    tile_rows, tile_cols, channels = pair_repr.shape
    bin_count = rel_embed.shape[0]
    reach_max = bin_count // 2 - 1
    first_row = lax.axis_index("row") * tile_rows
    first_col = lax.axis_index(("col", "samp")) * tile_cols
    row_ids = first_row + jnp.arange(tile_rows, dtype=jnp.int32)
    col_ids = first_col + jnp.arange(tile_cols, dtype=jnp.int32)
    row_chain = lax.dynamic_slice_in_dim(asym_id, first_row, tile_rows, 0)
    col_chain = lax.dynamic_slice_in_dim(asym_id, first_col, tile_cols, 0)
    offset = jnp.clip(row_ids[:, None] - col_ids[None, :], -reach_max, reach_max) + reach_max
    bin_ids = jnp.where(row_chain[:, None] == col_chain[None, :], offset, bin_count - 1)
    onehot = (
        bin_ids.reshape(-1)[:, None] == jnp.arange(bin_count, dtype=jnp.int32)[None, :]
    ).astype(jnp.bfloat16)
    summed = pair_repr.reshape(-1, channels).astype(jnp.float32) + jnp.dot(
        onehot, rel_embed, preferred_element_type=jnp.float32
    )
    normed = normalize(summed, pair_gain).astype(jnp.bfloat16)
    projected = lax.dot_general(
        bias_weight, normed, (((0,), (1,)), ((), ())), preferred_element_type=jnp.float32
    )
    return projected.reshape(bias_weight.shape[1], tile_rows, tile_cols)


def attend(queries, key_rows, value_rows, pair_bias, keymask, score_scale):
    head_count, query_count, key_count = pair_bias.shape
    model_width = queries.shape[-1]
    head_width = model_width // head_count
    query_h = queries.reshape(query_count, head_count, head_width)
    key_h = key_rows.reshape(key_count, head_count, head_width)
    value_h = value_rows.reshape(key_count, head_count, head_width)
    scores = (
        jnp.einsum("ihd,jhd->hij", query_h, key_h, preferred_element_type=jnp.float32) * score_scale
        + pair_bias
    )
    scores = jnp.where(keymask[None, None, :], scores, -1e30)
    row_max = jnp.max(scores, axis=-1, keepdims=True)
    weights = jnp.where(keymask[None, None, :], jnp.exp(scores - row_max), 0.0)
    row_total = jnp.sum(weights, axis=-1, keepdims=True)
    probs = (weights / row_total).astype(jnp.bfloat16)
    attended = jnp.einsum("hij,jhd->ihd", probs, value_h, preferred_element_type=jnp.float32)
    return attended.reshape(query_count, model_width).astype(jnp.bfloat16)


def per_device(
    pair_repr,
    asym_id,
    valid_len,
    rel_embed,
    pair_gain,
    bias_weight,
    tokens,
    token_gain,
    qkv_weight,
    out_weight,
):
    sample_count, token_rows, model_width = tokens.shape
    total_tokens = asym_id.shape[0]
    keymask = jnp.arange(total_tokens, dtype=jnp.int32) < valid_len[0]
    score_scale = 1.0 / math.sqrt(HEAD_DIM)
    bias_tile = bias_tile_of(pair_repr, asym_id, rel_embed, pair_gain, bias_weight)
    head_tile = lax.all_to_all(bias_tile, "row", split_axis=0, concat_axis=1, tiled=True)
    pair_bias = lax.all_gather(head_tile, ("col", "samp"), axis=2, tiled=True)

    def one_sample(sample_item):
        return attend(
            sample_item[0], sample_item[1], sample_item[2], pair_bias, keymask, score_scale
        )

    current = tokens
    normed = normalize(current.astype(jnp.float32), token_gain[0]).astype(jnp.bfloat16)
    layer_weight = qkv_weight[0]
    projected = jnp.einsum(
        "snc,pcw->psnw",
        lax.all_gather(normed, "row", axis=1, tiled=True),
        layer_weight,
        preferred_element_type=jnp.float32,
    ).astype(jnp.bfloat16)
    head_out = lax.map(one_sample, (projected[0], projected[1], projected[2]))
    attended = lax.all_to_all(head_out, "row", split_axis=1, concat_axis=2, tiled=True)
    flattened = attended.reshape(sample_count * token_rows, model_width)
    update = jnp.dot(
        flattened,
        lax.all_gather(out_weight[0], "row", axis=0, tiled=True),
        preferred_element_type=jnp.float32,
    )
    current = (
        current.astype(jnp.float32) + update.reshape(sample_count, token_rows, model_width)
    ).astype(jnp.bfloat16)
    return current


def solution(mesh):
    return jax.shard_map(
        per_device,
        mesh=mesh,
        in_specs=(
            P(("job", "row"), ("col", "samp"), None),
            P("job"),
            P("job"),
            P(),
            P(),
            P(),
            P(("job", "col", "samp"), "row", None),
            P(),
            P(None, None, None, "row"),
            P(None, "row", None),
        ),
        out_specs=P(("job", "col", "samp"), "row", None),
        check_vma=False,
    )
```

profile of v0, /device:TPU:0, one launch (start us, length us, event | category | flops | bytes accessed | tf_op | source)
XLA Modules:
  0.0 80.8 jit_solution(11071996184877069261)
XLA Ops:
  6.5 0.0 copy-start
  6.5 0.0 copy-start.2
  6.5 0.8 %fusion.27 = (s32[32]{0:T(128)S(1)}, s32[32]{0:T(128)S(1)}) fusion(s32[128]{0:T(128)} %param.13, s32[]{:T(128)S(6)} %select_n.24, s32[]{:T(128)S(6)} %select_n.25), kind=kLoop, calls=%fused_computation.52 | loop fusion | bytes 520 | tf_op jit(solution)/shard_map/dynamic_slice | solution.py:26
  7.4 0.1 add_select_fusion
  7.5 0.1 select_n.27
  7.5 1.0 %bitcast_convert_fusion = f32[1024,128]{1,0:T(8,128)S(1)} fusion(bf16[32,32,128]{2,1,0:T(8,128)(2,1)} %param.12), kind=kLoop, calls=%fused_computation.36 | loop fusion | flops 131072 | bytes 786432 | tf_op jit(solution)/shard_map/convert_element_type | solution.py:33
  8.5 0.0 copy-start.3
  8.5 0.0 copy-start.5
  8.5 0.2 copy.21
  8.7 0.0 copy-done.2
  8.8 1.0 %fusion.28 = (f32[1024]{0:T(1024)S(1)}, f32[1024,128]{0,1:T(8,128)S(1)}) fusion(f32[1024,128]{0,1:T(8,128)S(1)} %copy.21, bf16[128,128]{1,0:T(8,128)(2,1)S(1)} %copy-done.2, s32[1024]{0:T(1024)S(1)} %select_n.27), kind=kOutput, calls=%fused_computation.53 | convolution fusion | flops 33946624 | bytes 1089536 | tf_op jit(solution)/shard_map/dot_general | solution.py:33
  9.7 0.0 copy-start.1
  9.7 0.1 multiply_reduce_fusion
  9.8 0.0 copy-start.4
  9.8 0.0 copy-done.3
  9.9 0.0 copy-done.5
  9.9 0.2 convolution_bitcast_fusion
  10.1 0.1 reshape.112
  10.2 0.8 reshape.122
  11.0 6.3 %all-to-all-start = ((f32[4,1,4096]{2,1,0:T(1,128)}), f32[4,1,4096]{2,1,0:T(1,128)S(1)}, u32[]{:S(2)}, u32[]{:S(2)}) async-start(f32[4,1,4096]{2,1,0:T(1,128)} %reshape.122), calls=%async_computation | async-start | bytes 131072 | tf_op jit(solution)/shard_map/all_to_all | solution.py:80
  17.3 0.0 all-gather.3.cloned.1.call-start
  17.4 0.7 all-gather.3.cloned.1.call-update
  18.1 0.0 copy-done.1
  18.1 0.1 convert_reduce_fusion
  18.2 0.2 fusion.19
  18.4 0.0 copy-done.4
  18.4 0.1 fusion.21
  18.6 24.0 %all_gather.9 = bf16[4,128,768]{2,1,0:T(8,128)(2,1)S(1)} all-gather(bf16[4,32,768]{2,1,0:T(8,128)(2,1)S(1)} %fusion.21), channel_id=1, replica_groups=mesh['job'=2,'row'=4,'col'=2,'samp'=2] {'row'}, dimensions={1}, use_global_device_ids=true | all-gather | bytes 983040 | tf_op jit(solution)/shard_map/all_gather | solution.py:93
  42.6 0.0 copy-done
  42.6 0.6 fusion.10
  43.3 0.0 all-to-all-done
  43.3 0.5 broadcast.98
  43.8 0.8 %reduce.1 = f32[4,4096]{1,0:T(4,128)S(1)} reduce(f32[4,1,4096]{2,1,0:T(1,128)S(1)} %all-to-all-done, f32[]{:T(128)} %broadcast.98), dimensions={1}, to_apply=%all_to_all.24.reduce_sub_computation | reduce | bytes 131076 | tf_op jit(solution)/shard_map/all_to_all | solution.py:80
  44.7 0.1 reshape.123
  44.8 0.1 copy.22
  44.9 0.2 all_to_all.27
  45.1 5.8 %all_gather.10 = f32[4,128,128]{1,2,0:T(8,128)S(1)} all-gather(f32[4,128,32]{1,2,0:T(8,128)S(1)} %all_to_all.27), channel_id=1, replica_groups=mesh['job'=2,'row'=4,'col'=2,'samp'=2] {'col','samp'}, dimensions={2}, use_global_device_ids=true | all-gather | bytes 327680 | tf_op jit(solution)/shard_map/all_gather | solution.py:81
  50.9 5.3 %while.11 = (s32[]{:T(128)}, bf16[4,128,192]{1,2,0:T(8,128)(2,1)S(1)}, bf16[4,128,192]{1,2,0:T(8,128)(2,1)S(1)}, bf16[4,128,192]{1,2,0:T(8,128)(2,1)S(1)}, bf16[...) while((s32[]{:T(128)}, ...), condition=%wide.region_7.8_spmd.clone, body=%wide.region_4.7_spmd.clone.sunk | while | flops 13263744 | bytes 1643109 | solution.py:97
  50.9 0.6 iota_compare_fusion.4
  51.5 0.2 fusion.49
  51.8 0.1 fusion.50
  51.9 0.2 convolution_convert_fusion.3
  52.2 0.7 iota_compare_fusion.4
  52.9 0.2 fusion.49
  53.1 0.1 fusion.50
  53.3 0.2 convolution_convert_fusion.3
  53.6 0.7 iota_compare_fusion.4
  54.2 0.2 fusion.49
  54.5 0.1 fusion.50
  54.6 0.2 convolution_convert_fusion.3
  54.9 0.7 iota_compare_fusion.4
  55.6 0.2 fusion.49
  55.8 0.1 fusion.50
  55.9 0.2 convolution_convert_fusion.3
  56.2 0.2 copy.23
  56.4 14.7 %all_to_all.33 = bf16[4,128,192]{2,0,1:T(4,128)(2,1)S(1)} all-to-all(bf16[4,128,192]{2,0,1:T(4,128)(2,1)S(1)} %copy.23), channel_id=1, replica_groups=mesh['job'=2,'row'=4,'col'=2,'samp'=2] {'row'}, dimensions={1} | all-to-all | bytes 393216 | tf_op jit(solution)/shard_map/all_to_all | solution.py:98
  71.2 0.2 copy.25
  71.4 0.2 dot_general.26
  71.6 0.0 all-gather.3.cloned.1.call-done
  71.7 2.3 %fusion.12 = bf16[4,32,768]{2,1,0:T(8,128)(2,1)} fusion(bf16[4,32,768]{2,1,0:T(8,128)(2,1)S(1)} %dot_general.26, bf16[1,768,768]{2,1,0:T(8,128)(2,1)} %all-gather.3.cloned.1.call-done, bf16[4,32,768]{2,1,0:T(8,128)(2,1)S(1)} %copy-done.1), kind=kOutput, calls=%fused_computation.22 | convolution fusion | flops 151289856 | bytes 1769472 | tf_op jit(solution)/shard_map/dot_general | solution.py:100
  (21 shorter events, 0.3 us)
Async XLA Ops:
  6.5 36.1 %copy-start = (bf16[1,3,768,192]{2,3,1,0:T(8,128)(2,1)S(1)}, bf16[1,3,768,192]{2,3,1,0:T(8,128)(2,1)}, u32[]{:S(2)}) copy-start(bf16[1,3,768,192]{2,3,1,0:T(8,128)(2,1)} %param.20) | copy-start | bytes 2654212
  6.5 2.2 %copy-start.2 = (bf16[128,128]{1,0:T(8,128)(2,1)S(1)}, bf16[128,128]{1,0:T(8,128)(2,1)}, u32[]{:S(2)}) copy-start(bf16[128,128]{1,0:T(8,128)(2,1)} %param.15) | copy-start | bytes 98308
  8.5 1.3 %copy-start.3 = (bf16[128,16]{0,1:T(8,128)(2,1)S(1)}, bf16[128,16]{0,1:T(8,128)(2,1)}, u32[]{:S(2)}) copy-start(bf16[128,16]{0,1:T(8,128)(2,1)} %param.17) | copy-start | bytes 12292
  8.5 1.3 %copy-start.5 = (f32[128]{0:T(128)S(1)}, f32[128]{0:T(128)}, u32[]{:S(2)}) copy-start(f32[128]{0:T(128)} %param.16) | copy-start | bytes 1540
  9.7 8.4 %copy-start.1 = (bf16[4,32,768]{2,1,0:T(8,128)(2,1)S(1)}, bf16[4,32,768]{2,1,0:T(8,128)(2,1)}, u32[]{:S(2)}) copy-start(bf16[4,32,768]{2,1,0:T(8,128)(2,1)} %param.18) | copy-start | bytes 589828
  9.8 8.6 %copy-start.4 = (f32[1,768]{1,0:T(1,128)S(1)}, f32[1,768]{1,0:T(1,128)}, u32[]{:S(2)}) copy-start(f32[1,768]{1,0:T(1,128)} %param.19) | copy-start | bytes 9220
  11.0 32.3 %all-to-all-start = ((f32[4,1,4096]{2,1,0:T(1,128)}), f32[4,1,4096]{2,1,0:T(1,128)S(1)}, u32[]{:S(2)}, u32[]{:S(2)}) async-start(f32[4,1,4096]{2,1,0:T(1,128)} %reshape.122), calls=%async_computation | async-start | bytes 131072 | tf_op jit(solution)/shard_map/all_to_all | solution.py:80
  17.3 54.3 %all-gather.3.cloned.1.call-start = ((), (), s32[]{:S(2)}) async-start(), calls=%async_computation.2 | async-start | bytes 1474560 | tf_op jit(solution)/shard_map/all_gather | solution.py:102
Sparse Core Ops, SparseCore 0:
  19.7 35.6 all-gather.2
where the time goes:
time: 81.1 us; the launch traced here: 80.8 us
  blocking collectives  44.5 us (55%)
  between operations  13.6 us (17%)
  starting transfers between devices  6.35 us (8%)
  matrix products  6.03 us (7%)
  other arithmetic  5.46 us (7%)
  local copies, waits for them, and re-layouts  3.84 us (5%)
    all_gather x1, blocking collectives, per_device(): lax.all_gather(normed, 'row', axis=1, tiled=True)  24 us
    all_to_all x1, blocking collectives, per_device(): lax.all_to_all(head_out, 'row', split_axis=1, concat_axis=2, tiled=True)  14.7 us
    all_to_all x1, starting transfers between devices, per_device(): lax.all_to_all(bias_tile, 'row', split_axis=0, concat_axis=1, tiled=True)  6.35 us
    all_gather x1, blocking collectives, per_device(): pair_bias = lax.all_gather(head_tile, ('col', 'samp'), axis=2, tiled=True)  5.78 us
    lt x4, other arithmetic, per_device(): keymask = jnp.arange(total_tokens, dtype=jnp.int32) < valid_len[0]  2.61 us
    dot_general x1, matrix products, per_device(): jnp.dot(flattened, lax.all_gather(out_weight[0], 'row', axis=0, tiled=Tru...  2.28 us
  transfers between devices with their start and end apart: 2, of which 0 were waited for; matrix products, arithmetic and copies ran while one was open for 11% of the time, Pallas kernels for 0%

commit v1 on v0

--- a/solution.py
+++ b/solution.py
@@ -88,11 +88,45 @@
     current = tokens
     normed = normalize(current.astype(jnp.float32), token_gain[0]).astype(jnp.bfloat16)
     layer_weight = qkv_weight[0]
-    projected = jnp.einsum(
-        "snc,pcw->psnw",
-        lax.all_gather(normed, "row", axis=1, tiled=True),
-        layer_weight,
-        preferred_element_type=jnp.float32,
+
+    def _detail_tails(local_block, xin):
+        named_axis = "row"
+        wide_out = lax.axis_size(named_axis)
+        carry_out = lax.axis_index(named_axis)
+        piece_out, response, q_next = (wide_out, carry_out, local_block.shape[1])
+        mat_out, mixed_arr = ([], [])
+        even = value_now = local_block
+        ix = 0
+        while ix < piece_out // 2 + 1:
+            shaped = xin(even, (response - ix) % piece_out * q_next)
+            mat_out.append(shaped)
+            if 0 < ix < piece_out - piece_out // 2:
+                kept_arr = xin(value_now, (response + ix) % piece_out * q_next)
+                mixed_arr.append(kept_arr)
+            windows = []
+            b = 0
+            while b < piece_out:
+                windows.append((b, (b + 1) % piece_out))
+                b += 1
+            even = lax.ppermute(even, named_axis, windows)
+            pile = []
+            b = 0
+            while b < piece_out:
+                pile.append((b, (b - 1) % piece_out))
+                b += 1
+            value_now = lax.ppermute(value_now, named_axis, pile)
+            ix = ix + 1
+        return jnp.roll(
+            jnp.concatenate([*mat_out[::-1], *mixed_arr], axis=2),
+            shift=(response - piece_out // 2) * mat_out[0].shape[2],
+            axis=2,
+        )
+
+    projected = _detail_tails(
+        normed,
+        lambda part, offset_2: jnp.einsum(
+            "snc,pcw->psnw", part, layer_weight, preferred_element_type=jnp.float32
+        ),
     ).astype(jnp.bfloat16)
     head_out = lax.map(one_sample, (projected[0], projected[1], projected[2]))
     attended = lax.all_to_all(head_out, "row", split_axis=1, concat_axis=2, tiled=True)

time: 81.1 us -> 71.8 us (0.89)
  blocking collectives: 44.5 us -> 21.3 us
  starting transfers between devices: 6.35 us -> 10.8 us
  waiting for transfers between devices: 0.73 us -> 4.63 us
  other arithmetic: 5.46 us -> 9.07 us
  matrix products: 6.03 us -> 7.14 us
    all_gather x1 -> x0, blocking collectives: 24 us -> none  [per_device(): lax.all_gather(normed, 'row', axis=1, tiled=True)]
    ppermute x0 -> x3, starting transfers between devices: none -> 6.99 us  [the longest x2 5.13 us: _detail_tails(): even = lax.ppermute(even, named_axis, windows)]
    all_to_all x1, waiting for transfers between devices: 0.01 us -> 4.58 us  [per_device(): lax.all_to_all(bias_tile, 'row', split_axis=0, concat_axis=1, tiled=True)]
    all_to_all x1, starting transfers between devices: 6.35 us -> 3.86 us  [per_device(): lax.all_to_all(bias_tile, 'row', split_axis=0, concat_axis=1, tiled=True)]
    dot_general x1 -> x4, matrix products: 0.65 us -> 1.76 us  [per_device(): jnp.einsum('snc,pcw->psnw', part, layer_weight, preferred_element_type=jn...]
    reduce_sum x1, other arithmetic: 0.11 us -> 1.12 us  [normalize(): average = jnp.mean(values, axis=-1, keepdims=True)]
    convert_element_type x1, other arithmetic: 0.15 us -> 1.09 us  [per_device(): normalize(current.astype(jnp.float32), token_gain[0]).astype(jnp.bfloat16)]
    reduce_sum x2, other arithmetic: 0.26 us -> 1.19 us  [normalize(): variance = jnp.mean(centered * centered, axis=-1, keepdims=True)]
  transfers between devices with their start and end apart: 2 -> 5, of which waited for: 0 -> 1; matrix products, arithmetic and copies ran while one was open for 11% -> 20% of each run, Pallas kernels for 0% -> 0%
where the time goes in v1:
time: 71.8 us; the launch traced here: 71.4 us
  blocking collectives  21.3 us (30%)
  between operations  13.7 us (19%)
  starting transfers between devices  10.8 us (15%)
  other arithmetic  9.07 us (13%)
  matrix products  7.14 us (10%)
  waiting for transfers between devices  4.63 us (6%)
  local copies, waits for them, and re-layouts  4.44 us (6%)
    all_to_all x1, blocking collectives, per_device(): lax.all_to_all(head_out, 'row', split_axis=1, concat_axis=2, tiled=True)  15.5 us
    all_gather x1, blocking collectives, per_device(): pair_bias = lax.all_gather(head_tile, ('col', 'samp'), axis=2, tiled=True)  5.78 us
    ppermute x2, starting transfers between devices, _detail_tails(): even = lax.ppermute(even, named_axis, windows)  5.13 us
    all_to_all x1, waiting for transfers between devices, per_device(): lax.all_to_all(bias_tile, 'row', split_axis=0, concat_axis=1, tiled=True)  4.58 us
    all_to_all x1, starting transfers between devices, per_device(): lax.all_to_all(bias_tile, 'row', split_axis=0, concat_axis=1, tiled=True)  3.86 us
    lt x4, other arithmetic, per_device(): keymask = jnp.arange(total_tokens, dtype=jnp.int32) < valid_len[0]  2.61 us
    dot_general x1, matrix products, per_device(): jnp.dot(flattened, lax.all_gather(out_weight[0], 'row', axis=0, tiled=Tru...  2.28 us
    ppermute x1, starting transfers between devices, _detail_tails(): value_now = lax.ppermute(value_now, named_axis, pile)  1.86 us
  transfers between devices with their start and end apart: 5, of which 1 were waited for; matrix products, arithmetic and copies ran while one was open for 20% of the time, Pallas kernels for 0%

profile of v1, /device:TPU:0, one launch (start us, length us, event | category | flops | bytes accessed | tf_op | source)
XLA Modules:
  0.0 71.4 jit_solution(16313440501116665942)
XLA Ops:
  6.5 0.0 copy-start
  6.5 1.1 %convert_reduce_fusion = f32[4,32]{1,0:T(4,128)S(1)} fusion(bf16[4,32,768]{2,1,0:T(8,128)(2,1)} %param.18), kind=kLoop, calls=%fused_computation.32 | loop fusion | flops 196480 | bytes 197120 | tf_op jit(solution)/shard_map/reduce_sum | solution.py:12
  7.7 1.1 %fusion.20 = f32[4,32]{1,0:T(4,128)S(1)} fusion(bf16[4,32,768]{2,1,0:T(8,128)(2,1)} %param.18, f32[4,32]{1,0:T(4,128)S(1)} %broadcast_multiply_fusion.1), kind=kLoop, calls=%fused_computation.38 | loop fusion | flops 393088 | bytes 197632 | tf_op jit(solution)/shard_map/reduce_sum | solution.py:14
  8.8 0.7 reduce
  9.5 1.1 %fusion.22 = bf16[4,32,768]{2,1,0:T(8,128)(2,1)S(1)} fusion(bf16[4,32,768]{2,1,0:T(8,128)(2,1)} %param.18, f32[768]{0:T(1024)S(1)} %reduce, f32[4,32]{1,0:T(4,128)S(1)} %add_rsqrt_fusion.1, f32[4,32]{1,0:T(4,128)S(1)} %broadcast_multiply_fusion.1), kind=kLoop, calls=%fused_computation.40 | loop fusion | flops 491520 | bytes 397312 | tf_op jit(solution)/shard_map/convert_element_type | solution.py:89
  10.6 3.1 %collective-permute-start = (bf16[4,32,768]{2,1,0:T(8,128)(2,1)S(1)}, bf16[4,32,768]{2,1,0:T(8,128)(2,1)S(1)}, u32[]{:S(2)}, u32[]{:S(2)}) collective-permute-start(bf16[4,32,768]{2,1,0:T(8,128)(2,1)S(1)} %fusion.22), channel_id=1, source_target_pairs={{0,4},{4,8},{8,12},{12,0},{1,5},{5,9},{9,13},{13,1},{2,6},{6,10},{... | collective-permute-start | bytes 589832 | tf_op jit(solution)/shard_map/ppermute | solution.py:111
  13.7 0.8 %fusion.32 = (s32[32]{0:T(128)S(1)}, s32[32]{0:T(128)S(1)}) fusion(s32[128]{0:T(128)} %param.13, s32[]{:T(128)S(6)} %select_n.39, s32[]{:T(128)S(6)} %select_n.40), kind=kLoop, calls=%fused_computation.69 | loop fusion | bytes 520 | tf_op jit(solution)/shard_map/dynamic_slice | solution.py:26
  14.5 0.1 add_select_fusion
  14.6 0.1 select_n.42
  14.7 1.0 %bitcast_convert_fusion = f32[1024,128]{1,0:T(8,128)S(1)} fusion(bf16[32,32,128]{2,1,0:T(8,128)(2,1)} %param.12), kind=kLoop, calls=%fused_computation.44 | loop fusion | flops 131072 | bytes 786432 | tf_op jit(solution)/shard_map/convert_element_type | solution.py:33
  15.7 0.2 copy.27
  15.9 1.0 %fusion.33 = (f32[1024]{0:T(1024)S(1)}, f32[1024,128]{0,1:T(8,128)S(1)}) fusion(f32[1024,128]{0,1:T(8,128)S(1)} %copy.27, bf16[128,128]{1,0:T(8,128)(2,1)S(1)} %copy-done.2, s32[1024]{0:T(1024)S(1)} %select_n.42), kind=kOutput, calls=%fused_computation.70 | convolution fusion | flops 33946624 | bytes 1089536 | tf_op jit(solution)/shard_map/dot_general | solution.py:33
  16.9 0.1 multiply_reduce_fusion
  17.0 0.2 convolution_bitcast_fusion.4
  17.2 0.1 reshape.112
  17.3 0.8 %reshape.125 = f32[4,1,4096]{2,1,0:T(1,128)} reshape(f32[16,32,32]{2,1,0:T(8,128)S(1)} %reshape.112) | data formatting | bytes 131072
  18.1 3.9 %all-to-all-start = ((f32[4,1,4096]{2,1,0:T(1,128)}), f32[4,1,4096]{2,1,0:T(1,128)S(1)}, u32[]{:S(2)}, u32[]{:S(2)}) async-start(f32[4,1,4096]{2,1,0:T(1,128)} %reshape.125), calls=%async_computation | async-start | bytes 131072 | tf_op jit(solution)/shard_map/all_to_all | solution.py:80
  22.0 0.0 collective-permute-done
  22.0 2.0 %collective-permute-start.1 = (bf16[4,32,768]{2,1,0:T(8,128)(2,1)S(1)}, bf16[4,32,768]{2,1,0:T(8,128)(2,1)S(1)}, u32[]{:S(2)}, u32[]{:S(2)}) collective-permute-start(bf16[4,32,768]{2,1,0:T(8,128)(2,1)S(1)} %collective-permute-done), channel_id=1, source_target_pairs={{0,4},{4,8},{8,12},{12,0},{1,5},{5,9},{9,13},{13,1},{2,6},{6,10},{... | collective-permute-start | bytes 589832 | tf_op jit(solution)/shard_map/ppermute | solution.py:111
  24.0 1.9 %collective-permute-start.2 = (bf16[4,32,768]{2,1,0:T(8,128)(2,1)S(1)}, bf16[4,32,768]{2,1,0:T(8,128)(2,1)S(1)}, u32[]{:S(2)}, u32[]{:S(2)}) collective-permute-start(bf16[4,32,768]{2,1,0:T(8,128)(2,1)S(1)} %fusion.22), channel_id=1, source_target_pairs={{0,12},{4,0},{8,4},{12,8},{1,13},{5,1},{9,5},{13,9},{2,14},{6,2},{... | collective-permute-start | bytes 589832 | tf_op jit(solution)/shard_map/ppermute | solution.py:117
  25.9 0.0 all-gather.3.cloned.1.call-update
  25.9 4.6 %all-to-all-done = f32[4,1,4096]{2,1,0:T(1,128)S(1)} async-done(((f32[4,1,4096]{2,1,0:T(1,128)}), f32[4,1,4096]{2,1,0:T(1,128)S(1)}, u32[]{:S(2)}, u32[]{:S(2)}) %all-to-all-start) | async-done | bytes 65568 | tf_op jit(solution)/shard_map/all_to_all | solution.py:80
  30.5 0.5 broadcast.99
  31.0 0.8 %reduce.1 = f32[4,4096]{1,0:T(4,128)S(1)} reduce(f32[4,1,4096]{2,1,0:T(1,128)S(1)} %all-to-all-done, f32[]{:T(128)} %broadcast.99), dimensions={1}, to_apply=%all_to_all.24.reduce_sub_computation | reduce | bytes 131076 | tf_op jit(solution)/shard_map/all_to_all | solution.py:80
  31.9 0.1 reshape.126
  32.0 0.1 copy.28
  32.1 0.2 all_to_all.27
  32.3 5.8 %all_gather.6 = f32[4,128,128]{1,2,0:T(8,128)S(1)} all-gather(f32[4,128,32]{1,2,0:T(8,128)S(1)} %all_to_all.27), channel_id=1, replica_groups=mesh['job'=2,'row'=4,'col'=2,'samp'=2] {'col','samp'}, dimensions={2}, use_global_device_ids=true | all-gather | bytes 327680 | tf_op jit(solution)/shard_map/all_gather | solution.py:81
  38.1 0.0 collective-permute-done.1
  38.1 0.0 copy-done
  38.1 0.4 constant_dynamic-update-slice_fusion.8
  38.5 0.4 constant_dynamic-update-slice_fusion.7
  39.0 0.4 constant_dynamic-update-slice_fusion.6
  39.4 0.0 collective-permute-done.2
  39.4 0.4 constant_dynamic-update-slice_fusion.5
  40.0 0.1 dynamic-slice_convert_fusion
  40.1 0.1 slice_bitcast_fusion
  40.1 0.2 copy.29
  40.3 0.2 copy.30
  40.5 0.2 copy.31
  40.6 5.3 %while.11 = (s32[]{:T(128)}, bf16[4,128,192]{1,2,0:T(8,128)(2,1)S(1)}, bf16[4,128,192]{1,2,0:T(8,128)(2,1)S(1)}, bf16[4,128,192]{1,2,0:T(8,128)(2,1)S(1)}, bf16[...) while((s32[]{:T(128)}, ...), condition=%wide.region_7.8_spmd.clone, body=%wide.region_4.7_spmd.clone.sunk | while | flops 13263744 | bytes 1643109 | solution.py:131
  40.7 0.7 iota_compare_fusion.4
  41.3 0.2 fusion.54
  41.6 0.1 fusion.55
  41.7 0.2 convolution_convert_fusion.2
  42.0 0.7 iota_compare_fusion.4
  42.7 0.2 fusion.54
  42.9 0.1 fusion.55
  43.0 0.2 convolution_convert_fusion.2
  43.3 0.7 iota_compare_fusion.4
  44.0 0.2 fusion.54
  44.2 0.1 fusion.55
  44.4 0.2 convolution_convert_fusion.2
  44.7 0.7 iota_compare_fusion.4
  45.3 0.2 fusion.54
  45.6 0.1 fusion.55
  45.7 0.2 convolution_convert_fusion.2
  46.0 0.0 copy-start.1
  46.0 0.2 copy.32
  46.2 15.5 %all_to_all.33 = bf16[4,128,192]{2,0,1:T(4,128)(2,1)S(1)} all-to-all(bf16[4,128,192]{2,0,1:T(4,128)(2,1)S(1)} %copy.32), channel_id=1, replica_groups=mesh['job'=2,'row'=4,'col'=2,'samp'=2] {'row'}, dimensions={1} | all-to-all | bytes 393216 | tf_op jit(solution)/shard_map/all_to_all | solution.py:132
  61.8 0.2 copy.34
  62.0 0.2 dot_general.38
  62.2 0.0 all-gather.3.cloned.1.call-done
  62.2 2.3 %fusion.11 = bf16[4,32,768]{2,1,0:T(8,128)(2,1)} fusion(bf16[4,32,768]{2,1,0:T(8,128)(2,1)S(1)} %dot_general.38, bf16[1,768,768]{2,1,0:T(8,128)(2,1)} %all-gather.3.cloned.1.call-done, bf16[4,32,768]{2,1,0:T(8,128)(2,1)S(1)} %copy-done.1), kind=kOutput, calls=%fused_computation.25 | convolution fusion | flops 151289856 | bytes 1769472 | tf_op jit(solution)/shard_map/dot_general | solution.py:134
  (31 shorter events, 0.3 us)
Async XLA Ops:
  6.5 31.6 %copy-start = (bf16[1,3,768,192]{2,3,1,0:T(8,128)(2,1)S(1)}, bf16[1,3,768,192]{2,3,1,0:T(8,128)(2,1)}, u32[]{:S(2)}) copy-start(bf16[1,3,768,192]{2,3,1,0:T(8,128)(2,1)} %param.20) | copy-start | bytes 2654212
  6.5 9.4 %copy-start.2 = (bf16[128,128]{1,0:T(8,128)(2,1)S(1)}, bf16[128,128]{1,0:T(8,128)(2,1)}, u32[]{:S(2)}) copy-start(bf16[128,128]{1,0:T(8,128)(2,1)} %param.15) | copy-start | bytes 98308
  10.6 11.4 %collective-permute-start = (bf16[4,32,768]{2,1,0:T(8,128)(2,1)S(1)}, bf16[4,32,768]{2,1,0:T(8,128)(2,1)S(1)}, u32[]{:S(2)}, u32[]{:S(2)}) collective-permute-start(bf16[4,32,768]{2,1,0:T(8,128)(2,1)S(1)} %fusion.22), channel_id=1, source_target_pairs={{0,4},{4,8},{8,12},{12,0},{1,5},{5,9},{9,13},{13,1},{2,6},{6,10},{... | collective-permute-start | bytes 589832 | tf_op jit(solution)/shard_map/ppermute | solution.py:111
  14.7 2.3 %copy-start.3 = (bf16[128,16]{0,1:T(8,128)(2,1)S(1)}, bf16[128,16]{0,1:T(8,128)(2,1)}, u32[]{:S(2)}) copy-start(bf16[128,16]{0,1:T(8,128)(2,1)} %param.17) | copy-start | bytes 12292
  14.7 2.3 %copy-start.4 = (f32[128]{0:T(128)S(1)}, f32[128]{0:T(128)}, u32[]{:S(2)}) copy-start(f32[128]{0:T(128)} %param.16) | copy-start | bytes 1540
  18.1 12.4 %all-to-all-start = ((f32[4,1,4096]{2,1,0:T(1,128)}), f32[4,1,4096]{2,1,0:T(1,128)S(1)}, u32[]{:S(2)}, u32[]{:S(2)}) async-start(f32[4,1,4096]{2,1,0:T(1,128)} %reshape.125), calls=%async_computation | async-start | bytes 131072 | tf_op jit(solution)/shard_map/all_to_all | solution.py:80
  22.0 40.2 %all-gather.3.cloned.1.call-start = ((), (), s32[]{:S(2)}) async-start(), calls=%async_computation.2 | async-start | bytes 1474560 | tf_op jit(solution)/shard_map/all_gather | solution.py:136
  22.0 16.1 %collective-permute-start.1 = (bf16[4,32,768]{2,1,0:T(8,128)(2,1)S(1)}, bf16[4,32,768]{2,1,0:T(8,128)(2,1)S(1)}, u32[]{:S(2)}, u32[]{:S(2)}) collective-permute-start(bf16[4,32,768]{2,1,0:T(8,128)(2,1)S(1)} %collective-permute-done), channel_id=1, source_target_pairs={{0,4},{4,8},{8,12},{12,0},{1,5},{5,9},{9,13},{13,1},{2,6},{6,10},{... | collective-permute-start | bytes 589832 | tf_op jit(solution)/shard_map/ppermute | solution.py:111
  24.0 15.4 %collective-permute-start.2 = (bf16[4,32,768]{2,1,0:T(8,128)(2,1)S(1)}, bf16[4,32,768]{2,1,0:T(8,128)(2,1)S(1)}, u32[]{:S(2)}, u32[]{:S(2)}) collective-permute-start(bf16[4,32,768]{2,1,0:T(8,128)(2,1)S(1)} %fusion.22), channel_id=1, source_target_pairs={{0,12},{4,0},{8,4},{12,8},{1,13},{5,1},{9,5},{13,9},{2,14},{6,2},{... | collective-permute-start | bytes 589832 | tf_op jit(solution)/shard_map/ppermute | solution.py:117
  46.0 16.2 %copy-start.1 = (bf16[4,32,768]{2,1,0:T(8,128)(2,1)S(1)}, bf16[4,32,768]{2,1,0:T(8,128)(2,1)}, u32[]{:S(2)}) copy-start(bf16[4,32,768]{2,1,0:T(8,128)(2,1)} %param.18) | copy-start | bytes 589828
Sparse Core Ops, SparseCore 0:
  26.0 34.2 all-gather.2
